TPU v7x, 32 devices: a whole 2x2x4 slice. The times are simulated.
32 devices in a mesh: branch: 2 (over core), dp: 4 (over y, x), mp: 4 (over z).
Axes of the slice: x: 2, y: 2, z: 4, core: 2. Of those that a mesh axis runs over, the one named last changes fastest.
Arguments:
- unet_hidden: bfloat16 [8, 1280, 256], P(('branch', 'dp'), 'mp'), may hold values from -6 to 6
- control_hidden: bfloat16 [2, 2, 4, 1280, 256], P('branch', None, 'dp', 'mp'), may hold values from -6 to 6
- timesteps: int32 [2, 4], P(None, 'dp'), may hold values from 0 to 999
- control_scales: int32 [2, 2, 4], P('branch', None, 'dp'), may hold values from 1 to 16
- unet_time_first: bfloat16 [320, 1280], replicated, may hold values from -0.3125 to 0.3125
- unet_time_second: bfloat16 [1280, 1280], replicated, may hold values from -0.15625 to 0.15625
- unet_proj: bfloat16 [1280, 1280], P(None, 'mp'), may hold values from -0.15625 to 0.15625
- unet_conv_first: bfloat16 [9, 1280, 1280], P(None, 'mp'), may hold values from -0.0546875 to 0.0546875
- unet_conv_second: bfloat16 [9, 1280, 1280], P(None, 'mp'), may hold values from -0.0546875 to 0.0546875
- control_time_first: bfloat16 [2, 320, 1280], P('branch'), may hold values from -0.3125 to 0.3125
- control_time_second: bfloat16 [2, 1280, 1280], P('branch'), may hold values from -0.15625 to 0.15625
- control_proj: bfloat16 [2, 1280, 1280], P('branch', None, 'mp'), may hold values from -0.15625 to 0.15625
- control_conv_first: bfloat16 [2, 9, 1280, 1280], P('branch', None, 'mp'), may hold values from -0.0546875 to 0.0546875
- control_conv_second: bfloat16 [2, 9, 1280, 1280], P('branch', None, 'mp'), may hold values from -0.0546875 to 0.0546875
- zero_conv: bfloat16 [2, 1280, 1280], P('branch', 'mp'), may hold values from -0.15625 to 0.15625
Outputs:
- skip_out: bfloat16 [8, 1280, 256], P(('branch', 'dp'), 'mp')
All inputs are finite; a program needn't handle non-finite values.
Results may differ from a plain program's by a relative error of at most 0.018.
Values may be sent and summed in bfloat16 or wider, within the bound.
A program may use at most 128 MiB of HBM per device.

v0:
```python
import math

import jax
import jax.numpy as jnp
from jax import lax
from jax.sharding import PartitionSpec as P

C = 1280
TDIM = 320
GROUPS = 32
SIDE = 16


def sinusoid(step_ids):
    half_width = TDIM // 2
    frequency = jnp.exp(-math.log(10000.0) * jnp.arange(half_width, dtype=jnp.float32) / half_width)
    angles = step_ids.astype(jnp.float32)[:, None] * frequency[None, :]
    return jnp.concatenate([jnp.cos(angles), jnp.sin(angles)], axis=1)


def time_embed(step_ids, first_weight, second_weight):
    waves = sinusoid(step_ids).astype(jnp.bfloat16)
    middle = jax.nn.silu(jnp.dot(waves, first_weight, preferred_element_type=jnp.float32)).astype(
        jnp.bfloat16
    )
    embedded = jnp.dot(middle, second_weight, preferred_element_type=jnp.float32)
    return jax.nn.silu(embedded).astype(jnp.bfloat16)


def norm_silu(values):
    image_count, width, pixels = values.shape
    group_size = C // GROUPS
    grouped = values.reshape(image_count, width // group_size, group_size, pixels)
    group_mean = jnp.mean(grouped, axis=(2, 3), keepdims=True)
    centered = grouped - group_mean
    group_var = jnp.mean(centered * centered, axis=(2, 3), keepdims=True)
    normed = centered * lax.rsqrt(group_var + 1e-05)
    return jax.nn.silu(normed).reshape(image_count, width, pixels)


def conv_taps(activation, weight, einsum_form):
    image_count, width, pixels = activation.shape
    image_grid = activation.reshape(image_count, width, SIDE, SIDE)
    padded = jnp.pad(image_grid, ((0, 0), (0, 0), (1, 1), (1, 1)))
    accum_sum = None
    for tap_index in range(9):
        row_shift = tap_index // 3
        col_shift = tap_index % 3
        window = padded[:, :, row_shift : row_shift + SIDE, col_shift : col_shift + SIDE].reshape(
            image_count, width, pixels
        )
        term = jnp.einsum(
            einsum_form, weight[tap_index], window, preferred_element_type=jnp.float32
        )
        accum_sum = term if accum_sum is None else accum_sum + term
    return accum_sum


def resnet_block(hidden, conv_first, conv_second, time_proj, time_act, for_unet):
    start_sum = jnp.zeros((hidden.shape[0], conv_first.shape[1], hidden.shape[2]), jnp.float32)
    start_sum = (
        start_sum + jnp.dot(time_act, time_proj, preferred_element_type=jnp.float32)[:, :, None]
    )
    operand = norm_silu(hidden.astype(jnp.float32)).astype(jnp.bfloat16)

    def fold_first(running, shard_piece):
        return running + conv_taps(shard_piece, conv_first, "oc,bcp->bop")

    if for_unet:
        inner_sum = fold_first(start_sum, lax.all_gather(operand, "mp", axis=1, tiled=True))
    else:
        inner_sum = fold_first(start_sum, lax.all_gather(operand, "mp", axis=1, tiled=True))
    second_act = norm_silu(inner_sum).astype(jnp.bfloat16)
    partial_sum = conv_taps(second_act, conv_second, "co,bcp->bop")
    if for_unet:
        outer_sum = lax.psum_scatter(
            partial_sum.astype(jnp.bfloat16), "mp", scatter_dimension=1, tiled=True
        ).astype(jnp.float32)
    else:
        outer_sum = lax.psum_scatter(
            partial_sum.astype(jnp.bfloat16), "mp", scatter_dimension=1, tiled=True
        ).astype(jnp.float32)
    return hidden.astype(jnp.float32) + outer_sum


def shards(
    unet_hidden,
    control_hidden,
    timesteps,
    control_scales,
    unet_time_first,
    unet_time_second,
    unet_proj,
    unet_conv_first,
    unet_conv_second,
    control_time_first,
    control_time_second,
    control_proj,
    control_conv_first,
    control_conv_second,
    zero_conv,
):
    model_ways = lax.axis_size("mp")
    halves, image_count = timesteps.shape
    local_width = unet_hidden.shape[1]
    pixels = unet_hidden.shape[2]
    own_steps = lax.dynamic_index_in_dim(timesteps, lax.axis_index("branch"), 0, keepdims=False)
    time_act = time_embed(own_steps, unet_time_first, unet_time_second)
    unet_out = resnet_block(
        unet_hidden, unet_conv_first, unet_conv_second, unet_proj, time_act, True
    )
    time_act = time_embed(
        timesteps.reshape(halves * image_count), control_time_first[0], control_time_second[0]
    )
    stacked = control_hidden[0].reshape(halves * image_count, local_width, pixels)
    copy_out = resnet_block(
        stacked, control_conv_first[0], control_conv_second[0], control_proj[0], time_act, False
    ).astype(jnp.bfloat16)
    weight_blocks = zero_conv[0].reshape(local_width, model_ways, local_width)
    shaped = copy_out.reshape(halves, image_count, local_width, pixels)
    zero_terms = jnp.einsum(
        "ckd,hbcp->hkbdp", weight_blocks, shaped, preferred_element_type=jnp.float32
    )
    scale_factor = control_scales[0].astype(jnp.float32) / 8.0
    zero_terms = zero_terms * scale_factor[:, None, :, None, None]
    merged = zero_terms.reshape(halves * model_ways, image_count, local_width, pixels)
    residual = lax.psum_scatter(
        merged.astype(jnp.bfloat16), ("branch", "mp"), scatter_dimension=0, tiled=True
    ).astype(jnp.float32)[0]
    return (unet_out + residual).astype(jnp.bfloat16)


def solution(mesh):
    in_specs = (
        P(("branch", "dp"), "mp", None),
        P("branch", None, "dp", "mp", None),
        P(None, "dp"),
        P("branch", None, "dp"),
        P(),
        P(),
        P(None, "mp"),
        P(None, "mp", None),
        P(None, "mp", None),
        P("branch", None, None),
        P("branch", None, None),
        P("branch", None, "mp"),
        P("branch", None, "mp", None),
        P("branch", None, "mp", None),
        P("branch", "mp", None),
    )
    out_specs = P(("branch", "dp"), "mp", None)
    return jax.shard_map(shards, mesh=mesh, in_specs=in_specs, out_specs=out_specs, check_vma=False)
```

profile of v0, /device:TPU:0, one launch (start us, length us, event | category | flops | bytes accessed | tf_op | source)
XLA Modules:
  0.0 215.8 jit_solution(13136766995914639169)
XLA Ops:
  6.5 1.3 convert_reduce_fusion
  8.2 1.3 fusion.106
  9.8 2.0 fusion.103
  11.9 1.1 convert_reduce_fusion.1
  13.3 1.1 fusion.116
  14.8 1.1 fusion.115
  15.9 27.8 %all_gather.6 = bf16[1,1280,256]{2,1,0:T(8,128)(2,1)} all-gather(bf16[1,320,256]{2,1,0:T(8,128)(2,1)S(1)} %fusion.115), channel_id=1, replica_groups=mesh['branch'=2,'dp'=4,'mp'=4] {'mp'}, dimensions={1}, use_global_device_ids=true | all-gather | bytes 819200 | tf_op jit(solution)/shard_map/all_gather | solution.py:70
  43.8 2.2 %copy.50 = bf16[1,1280,256]{1,2,0:T(8,128)(2,1)} copy(bf16[1,1280,256]{2,1,0:T(8,128)(2,1)} %all_gather.6) | data formatting | bytes 1310720 | tf_op jit(solution)/shard_map/all_gather | solution.py:70
  45.9 4.9 %pad_slice_fusion.8 = (bf16[1,1280,16,16]{1,3,2,0:T(8,128)(2,1)}, bf16[1,1280,16,16]{1,3,2,0:T(8,128)(2,1)}, bf16[1,1280,16,16]{1,3,2,0:T(8,128)(2,1)}, bf16[1,1...) fusion(bf16[1,1280,16,16]{1,3,2,0:T(8,128)(2,1)} %bitcast.349), kind=kLoop, calls=%fused_computation.32 | loop fusion | bytes 5898240 | tf_op jit(solution)/shard_map/slice | solution.py:49
  50.9 2.3 %fusion.57 = f32[256,320]{0,1:T(8,128)} fusion(bf16[1280,256]{0,1:T(8,128)(2,1)S(1)} %bitcast.375, bf16[9,320,1280]{2,1,0:T(8,128)(2,1)} %param.22), kind=kOutput, calls=%fused_computation.118 | convolution fusion | flops 209715200 | bytes 1802240 | tf_op jit(solution)/shard_map/oc,bcp->bop/dot_general | solution.py:52
  53.2 2.3 %fusion.51 = f32[256,320]{0,1:T(8,128)} fusion(bf16[1280,256]{0,1:T(8,128)(2,1)S(1)} %bitcast.374, bf16[9,320,1280]{2,1,0:T(8,128)(2,1)} %param.22), kind=kOutput, calls=%fused_computation.112 | convolution fusion | flops 209715200 | bytes 1802240 | tf_op jit(solution)/shard_map/oc,bcp->bop/dot_general | solution.py:52
  56.8 1.4 convolution_reduce_fusion.1
  58.9 1.6 convolution_add_fusion.29
  60.6 1.6 convolution_add_fusion.28
  62.2 1.6 convolution_add_fusion.27
  63.9 1.6 fusion.10
  65.5 1.7 convolution_add_fusion.26
  67.2 1.5 convolution_add_fusion.25
  69.1 2.5 %fusion.148 = (f32[320]{0:T(512)S(1)}, f32[1,256,320]{1,2,0:T(8,128)}) fusion(f32[256,320]{0,1:T(8,128)S(1)} %convolution_add_fusion.25, bf16[1280,256]{0,1:T(8,128)(2,1)S(1)} %bitcast.373, bf16[9,320,1280]{2,1,0:T(8,128)(2,1)} %param.22, f32[320]{0:T(512)S(1)} %convolution_reduce_fusion.2), kind=kOutput, calls=%fused_computation.235 | convolution fusion | flops 209960640 | bytes 2132480 | tf_op jit(solution)/shard_map/oc,bcp->bop/dot_general | solution.py:52
  71.9 1.2 multiply_reduce_fusion.1
  73.5 1.2 fusion.125
  75.5 3.2 %pad_slice_fusion.24 = (bf16[1,320,16,16]{1,3,2,0:T(8,128)(2,1)}, bf16[1,320,16,16]{1,3,2,0:T(8,128)(2,1)}, bf16[1,320,16,16]{1,3,2,0:T(8,128)(2,1)}, bf16[1,320...) fusion(bf16[1,320,16,16]{1,3,2,0:T(8,128)(2,1)} %bitcast.372), kind=kLoop, calls=%fused_computation.171 | loop fusion | bytes 1474560 | tf_op jit(solution)/shard_map/slice | solution.py:49
  78.8 1.4 fusion.136
  80.3 1.9 fusion.34
  82.2 2.5 %copy.62 = bf16[2,1280,256]{1,2,0:T(8,128)(2,1)} copy(bf16[2,1280,256]{2,1,0:T(8,128)(2,1)} %all-gather.2.cloned.1.call-done) | data formatting | bytes 2621440 | tf_op jit(solution)/shard_map/all_gather | solution.py:72
  84.6 8.2 %pad_slice_fusion = (bf16[2,1280,16,16]{1,3,2,0:T(8,128)(2,1)S(1)}, bf16[2,1280,16,16]{1,3,2,0:T(8,128)(2,1)S(1)}, bf16[2,1280,16,16]{1,3,2,0:T(8,128)(2,1)S(1)}...) fusion(bf16[2,1280,16,16]{1,3,2,0:T(8,128)(2,1)} %bitcast.341), kind=kLoop, calls=%fused_computation | loop fusion | bytes 11796480 | tf_op jit(solution)/shard_map/slice | solution.py:49
  92.8 1.8 fusion.32
  101.8 2.2 %fusion.21 = f32[2,256,1280]{1,2,0:T(8,128)S(1)} fusion(bf16[2,320,256]{1,2,0:T(8,128)(2,1)S(1)} %bitcast.357, bf16[1,9,320,1280]{3,2,1,0:T(8,128)(2,1)} %param.28), kind=kOutput, calls=%fused_computation.82 | convolution fusion | flops 419430400 | bytes 3768320 | tf_op jit(solution)/shard_map/co,bcp->bop/dot_general | solution.py:52
  104.0 2.0 convolution_add_fusion.7
  106.1 0.9 convolution_add_fusion.6
  109.7 0.9 convolution_add_fusion.2
  110.6 0.9 convolution_add_fusion.1
  111.5 2.0 fusion.3
  113.8 1.7 fusion.46
  115.6 1.7 convolution_add_fusion.15
  117.3 1.7 convolution_add_fusion.14
  119.0 1.7 convolution_add_fusion.13
  120.8 1.7 convolution_add_fusion.12
  122.5 1.7 convolution_add_fusion.11
  124.3 1.7 convolution_add_fusion.10
  126.1 1.7 convolution_add_fusion.9
  127.8 2.6 %fusion.6 = bf16[1,1280,256]{2,1,0:T(8,128)(2,1)} fusion(f32[256,1280]{0,1:T(8,128)S(1)} %convolution_add_fusion.9, bf16[320,256]{0,1:T(8,128)(2,1)S(1)} %bitcast.370, bf16[9,320,1280]{2,1,0:T(8,128)(2,1)} %param.23), kind=kOutput, calls=%fused_computation.31 | convolution fusion | flops 210370560 | bytes 2949120 | tf_op jit(solution)/shard_map/co,bcp->bop/dot_general | solution.py:52
  130.5 2.4 %copy.125 = bf16[1,320,1280]{1,2,0:T(8,128)(2,1)} copy(bf16[1,320,1280]{2,1,0:T(8,128)(2,1)} %param.29) | data formatting | bytes 1638400 | tf_op jit(solution)/shard_map/reshape;squeeze | solution.py:119
  132.9 12.9 %reduce-scatter.6.cloned.1.call-done = bf16[2,320,256]{2,1,0:T(8,128)(2,1)} async-done(((bf16[2,1280,256]{2,1,0:T(8,128)(2,1)}), bf16[2,320,256]{2,1,0:T(8,128)(2,1)}) %reduce-scatter.6.cloned.1.call-update) | async-done | bytes 327696 | tf_op jit(solution)/shard_map/reduce_scatter | solution.py:80
  145.8 3.3 %fusion.4 = bf16[2,1,256,4,320]{2,4,3,0,1:T(8,128)(2,1)} fusion(bf16[320,4,320,1]{0,2,1,3:T(8,128)(2,1)} %bitcast.363, f32[2]{0:T(128)S(1)} %multiply_bitcast_fusion, bf16[2,320,256]{2,1,0:T(8,128)(2,1)} %reduce-scatter.6.cloned.1.call-done, bf16[1,2,1,320,256]{4,3,2,1,0:T(8,128)(2,1)} %param.16), kind=kOutput, calls=%fused_computation.29 | convolution fusion | flops 421396480 | bytes 2785288 | tf_op jit(solution)/shard_map/ckd,hbcp->hkbdp/dot_general | solution.py:121
  149.1 20.2 %reduce-scatter.4.cloned.1.call-done = bf16[1,320,256]{2,1,0:T(8,128)(2,1)} async-done(((bf16[1,1280,256]{2,1,0:T(8,128)(2,1)}), bf16[1,320,256]{2,1,0:T(8,128)(2,1)}) %reduce-scatter.4.cloned.1.call-update) | async-done | bytes 163856 | tf_op jit(solution)/shard_map/reduce_scatter | solution.py:76
  169.3 38.2 %reduce-scatter.8.cloned.1.call-done = bf16[1,1,320,256]{3,2,1,0:T(8,128)(2,1)} async-done(((bf16[8,1,320,256]{3,2,1,0:T(8,128)(2,1)}), bf16[1,1,320,256]{3,2,1,0:T(8,128)(2,1)}) %reduce-scatter.8.cloned.1.call-update) | async-done | bytes 163856 | tf_op jit(solution)/shard_map/reduce_scatter | solution.py:127
  207.6 1.7 fusion.118
  (139 shorter events, 15.6 us)
Async XLA Ops:
  6.5 51.7 %copy-start = (bf16[1280,1280]{1,0:T(8,128)(2,1)S(1)}, bf16[1280,1280]{1,0:T(8,128)(2,1)}, u32[]{:S(2)}) copy-start(bf16[1280,1280]{1,0:T(8,128)(2,1)} %param.20) | copy-start | bytes 9830404
  6.5 75.6 %all-gather.2.cloned.1.call-start = ((), (), s32[]{:S(2)}) async-start(), calls=%async_computation.4 | async-start | bytes 1638400 | tf_op jit(solution)/shard_map/all_gather | solution.py:72
  11.8 133.9 %reduce-scatter.6.cloned.1.call-start = ((), (), s32[]{:S(2)}) async-start(), calls=%async_computation.5 | async-start | bytes 1638400 | tf_op jit(solution)/shard_map/reduce_scatter | solution.py:80
  50.9 4.6 %copy-start.23 = (s32[2,1]{0,1:T(1,128)S(1)}, s32[2,1]{0,1:T(1,128)}, u32[]{:S(2)}) copy-start(s32[2,1]{0,1:T(1,128)} %param.17) | copy-start | bytes 28
  55.5 3.4 %copy-start.10 = (bf16[1,1280,16,16]{1,3,2,0:T(8,128)(2,1)S(1)}, bf16[1,1280,16,16]{1,3,2,0:T(8,128)(2,1)}, u32[]{:S(2)}) copy-start(bf16[1,1280,16,16]{1,3,2,0:T(8,128)(2,1)} %get-tuple-element.14) | copy-start | bytes 1966084
  55.5 3.4 %copy-start.22 = (f32[256,320]{0,1:T(8,128)S(1)}, f32[256,320]{0,1:T(8,128)}, u32[]{:S(2)}) copy-start(f32[256,320]{0,1:T(8,128)} %fusion.57) | copy-start | bytes 983044
  58.3 2.3 %copy-start.9 = (bf16[1,1280,16,16]{1,3,2,0:T(8,128)(2,1)S(1)}, bf16[1,1280,16,16]{1,3,2,0:T(8,128)(2,1)}, u32[]{:S(2)}) copy-start(bf16[1,1280,16,16]{1,3,2,0:T(8,128)(2,1)} %get-tuple-element.15) | copy-start | bytes 1966084
  58.8 3.4 %copy-start.8 = (bf16[1,1280,16,16]{1,3,2,0:T(8,128)(2,1)S(1)}, bf16[1,1280,16,16]{1,3,2,0:T(8,128)(2,1)}, u32[]{:S(2)}) copy-start(bf16[1,1280,16,16]{1,3,2,0:T(8,128)(2,1)} %get-tuple-element.16) | copy-start | bytes 1966084
  60.5 3.3 %copy-start.2 = (bf16[1,1280,256]{2,1,0:T(8,128)(2,1)S(1)}, bf16[1,1280,256]{2,1,0:T(8,128)(2,1)}, u32[]{:S(2)}) copy-start(bf16[1,1280,256]{2,1,0:T(8,128)(2,1)} %all_gather.6) | copy-start | bytes 1966084
  60.5 3.3 %copy-start.21 = (f32[256,320]{0,1:T(8,128)S(1)}, f32[256,320]{0,1:T(8,128)}, u32[]{:S(2)}) copy-start(f32[256,320]{0,1:T(8,128)} %fusion.51) | copy-start | bytes 983044
  62.2 3.3 %copy-start.7 = (bf16[1,1280,16,16]{1,3,2,0:T(8,128)(2,1)S(1)}, bf16[1,1280,16,16]{1,3,2,0:T(8,128)(2,1)}, u32[]{:S(2)}) copy-start(bf16[1,1280,16,16]{1,3,2,0:T(8,128)(2,1)} %get-tuple-element.18) | copy-start | bytes 1966084
  63.9 3.3 %copy-start.6 = (bf16[1,1280,16,16]{1,3,2,0:T(8,128)(2,1)S(1)}, bf16[1,1280,16,16]{1,3,2,0:T(8,128)(2,1)}, u32[]{:S(2)}) copy-start(bf16[1,1280,16,16]{1,3,2,0:T(8,128)(2,1)} %get-tuple-element.19) | copy-start | bytes 1966084
  65.5 3.3 %copy-start.11 = (bf16[1280,320]{0,1:T(8,128)(2,1)S(1)}, bf16[1280,320]{0,1:T(8,128)(2,1)}, u32[]{:S(2)}) copy-start(bf16[1280,320]{0,1:T(8,128)(2,1)} %param.21) | copy-start | bytes 2457604
  65.5 3.6 %copy-start.20 = (bf16[1,1280,16,16]{1,3,2,0:T(8,128)(2,1)S(1)}, bf16[1,1280,16,16]{1,3,2,0:T(8,128)(2,1)}, u32[]{:S(2)}) copy-start(bf16[1,1280,16,16]{1,3,2,0:T(8,128)(2,1)} %get-tuple-element.13) | copy-start | bytes 1966084
  69.1 11.2 %copy-start.4 = (bf16[1,1280,1280]{2,1,0:T(8,128)(2,1)S(1)}, bf16[1,1280,1280]{2,1,0:T(8,128)(2,1)}, u32[]{:S(2)}) copy-start(bf16[1,1280,1280]{2,1,0:T(8,128)(2,1)} %param.25) | copy-start | bytes 9830404
  84.6 10.0 %slice-start.2 = ((s8[7372800]{0:T(1024)(128)(4,1)}), s8[4194304]{0:T(1024)(128)(4,1)S(1)}, s32[]{:S(2)}) async-start(s8[7372800]{0:T(1024)(128)(4,1)} %bitcast.342), calls=%async_computation.9 | async-start | bytes 8388608
  84.6 10.0 %slice-start.3 = ((s8[7372800]{0:T(1024)(128)(4,1)}), s8[3178496]{0:T(1024)(128)(4,1)S(1)}, s32[]{:S(2)}) async-start(s8[7372800]{0:T(1024)(128)(4,1)} %bitcast.342), calls=%async_computation.10 | async-start | bytes 6356992
  95.9 1.3 copy-start.3
  101.4 4.7 %slice-start = ((s8[7372800]{0:T(1024)(128)(4,1)}), s8[3178496]{0:T(1024)(128)(4,1)S(1)}, s32[]{:S(2)}) async-start(s8[7372800]{0:T(1024)(128)(4,1)} %bitcast.334), calls=%async_computation.7 | async-start | bytes 6356992
  101.7 4.3 %slice-start.1 = ((s8[7372800]{0:T(1024)(128)(4,1)}), s8[4194304]{0:T(1024)(128)(4,1)S(1)}, s32[]{:S(2)}) async-start(s8[7372800]{0:T(1024)(128)(4,1)} %bitcast.334), calls=%async_computation.8 | async-start | bytes 8388608
  111.5 2.3 %copy-start.19 = (bf16[1,320,16,16]{1,3,2,0:T(8,128)(2,1)S(1)}, bf16[1,320,16,16]{1,3,2,0:T(8,128)(2,1)}, u32[]{:S(2)}) copy-start(bf16[1,320,16,16]{1,3,2,0:T(8,128)(2,1)} %get-tuple-element.36) | copy-start | bytes 491524
  113.5 2.1 copy-start.17
  113.5 55.8 %reduce-scatter.4.cloned.1.call-start = ((), (), s32[]{:S(2)}) async-start(), calls=%async_computation.3 | async-start | bytes 819200 | tf_op jit(solution)/shard_map/reduce_scatter | solution.py:76
  113.8 3.5 %copy-start.16 = (bf16[1,320,16,16]{1,3,2,0:T(8,128)(2,1)S(1)}, bf16[1,320,16,16]{1,3,2,0:T(8,128)(2,1)}, u32[]{:S(2)}) copy-start(bf16[1,320,16,16]{1,3,2,0:T(8,128)(2,1)} %get-tuple-element.31) | copy-start | bytes 491524
  117.3 1.8 copy-start.15
  120.8 1.8 copy-start.14
  122.5 1.8 copy-start.13
  124.3 1.8 copy-start.12
  126.0 1.8 copy-start.18
  127.8 5.0 %copy-start.24 = (s32[1,2,1]{1,2,0:T(1,128)S(1)}, s32[1,2,1]{1,2,0:T(1,128)}, u32[]{:S(2)}) copy-start(s32[1,2,1]{1,2,0:T(1,128)} %param.18) | copy-start | bytes 28
  130.4 77.1 %reduce-scatter.8.cloned.1.call-start = ((), (), s32[]{:S(2)}) async-start(), calls=%async_computation.6 | async-start | bytes 1474560 | tf_op jit(solution)/shard_map/reduce_scatter | solution.py:127
  130.5 78.8 %copy-start.1 = (bf16[1280,1280]{1,0:T(8,128)(2,1)S(1)}, bf16[1280,1280]{1,0:T(8,128)(2,1)}, u32[]{:S(2)}) copy-start(bf16[1280,1280]{1,0:T(8,128)(2,1)} %param.20) | copy-start | bytes 9830404
  132.9 74.7 %copy-start.5 = (bf16[1,320,256]{2,1,0:T(8,128)(2,1)S(1)}, bf16[1,320,256]{2,1,0:T(8,128)(2,1)}, u32[]{:S(2)}) copy-start(bf16[1,320,256]{2,1,0:T(8,128)(2,1)} %param.15) | copy-start | bytes 491524
Sparse Core Ops, SparseCore 0:
  11.9 42.2 all-gather.1
  113.6 32.0 reduce-scatter.5
  148.0 21.2 reduce-scatter.3
  171.5 36.0 reduce-scatter.7
where the time goes:
time: 217 us; the launch traced here: 216 us
  waiting for transfers between devices  71.4 us (33%)
  matrix products  60.6 us (28%)
  blocking collectives  27.8 us (13%)
  local copies, waits for them, and re-layouts  26.8 us (12%)
  other arithmetic  15 us (7%)
  between operations  13.9 us (6%)
    dot_general x36, matrix products, conv_taps(): jnp.einsum(einsum_form, weight[tap_index], window, preferred_element_type...  51.6 us
    reduce_scatter x1, waiting for transfers between devices, shards(): lax.psum_scatter(merged.astype(jnp.bfloat16), ('branch', 'mp'), scatter_d...  38.2 us
    reduce_scatter x2, waiting for transfers between devices, resnet_block(): lax.psum_scatter(partial_sum.astype(jnp.bfloat16), 'mp', scatter_dimensio...  33.1 us
    all_gather x1, blocking collectives, resnet_block(): lax.all_gather(operand, 'mp', axis=1, tiled=True)  27.8 us
    slice x4, local copies, waits for them, and re-layouts, conv_taps(): padded[:, :, row_shift:row_shift + SIDE, col_shift:col_shift + SIDE]  16.7 us
    all_gather x2, local copies, waits for them, and re-layouts, resnet_block(): lax.all_gather(operand, 'mp', axis=1, tiled=True)  4.63 us
  transfers between devices with their start and end apart: 4, of which 3 were waited for; matrix products, arithmetic and copies ran while one was open for 30% of the time, Pallas kernels for 0%

commit v1 on v0

v1 whole, which is shorter than its diff:
```python
import functools
import math

import jax
import jax.numpy as jnp
from jax import lax
from jax.experimental import pallas as pl
from jax.experimental.pallas import tpu as pltpu
from jax.sharding import PartitionSpec as P

TDIM = 320
GROUP = 40
SIDE = 16
MESH = pl.DeviceIdType.MESH


def sinusoid(step_ids):
    half_width = TDIM // 2
    frequency = jnp.exp(-math.log(10000.0) * jnp.arange(half_width, dtype=jnp.float32) / half_width)
    angles = step_ids.astype(jnp.float32)[:, None] * frequency[None, :]
    return jnp.concatenate([jnp.cos(angles), jnp.sin(angles)], axis=1)


def time_embed(waves, first_weight, second_weight):
    middle = jax.nn.silu(jnp.dot(waves, first_weight, preferred_element_type=jnp.float32)).astype(
        jnp.bfloat16
    )
    embedded = jnp.dot(middle, second_weight, preferred_element_type=jnp.float32)
    return jax.nn.silu(embedded).astype(jnp.bfloat16)


def norm_silu(values):
    width, pixels = values.shape
    grouped = values.reshape(width // GROUP, GROUP, pixels)
    count = 1.0 / (GROUP * pixels)
    mean = jnp.sum(jnp.sum(grouped, axis=1, keepdims=True), axis=2, keepdims=True) * count
    centered = grouped - mean
    var = jnp.sum(jnp.sum(centered * centered, axis=1, keepdims=True), axis=2, keepdims=True) * count
    normed = centered * lax.rsqrt(var + 1e-05)
    return jax.nn.silu(normed).reshape(width, pixels)


def kernel(
    ways,
    unet_hidden,
    control_hidden,
    start,
    scale,
    first_u,
    second_u,
    first_c,
    second_c,
    zero,
    out,
    w1u,
    w2u,
    w1c,
    w2c,
    wz,
    gathered,
    inner,
    flipped,
    total_c,
    total_u,
    sends,
    lands,
    swap_out,
    swap_in,
    load_sem,
    ag_send,
    ag_recv,
    rs_send,
    rs_recv,
    swap_send,
    swap_recv,
):
    branch = lax.axis_index("branch")
    dp = lax.axis_index("dp")
    me = lax.axis_index("mp")
    width, pixels = unet_hidden.shape[1], unet_hidden.shape[2]
    channels = ways * width

    loads = [
        pltpu.make_async_copy(src, dst, load_sem.at[i])
        for i, (src, dst) in enumerate(
            ((first_c, w1c), (second_c, w2c), (first_u, w1u), (second_u, w2u), (zero, wz))
        )
    ]
    for load in loads:
        load.start()

    barrier = pltpu.get_barrier_semaphore()
    for d in range(1, ways):
        pl.semaphore_signal(
            barrier, inc=1, device_id=(branch, dp, lax.rem(me + d, ways)), device_id_type=MESH
        )
    pl.semaphore_signal(barrier, inc=1, device_id=(1 - branch, dp, me), device_id_type=MESH)

    def ag_copy(unit, d, slot):
        return pltpu.make_async_remote_copy(
            src_ref=gathered.at[unit, slot],
            dst_ref=gathered.at[unit, slot],
            send_sem=ag_send.at[unit, d - 1],
            recv_sem=ag_recv.at[unit, d - 1],
            device_id=(branch, dp, lax.rem(me + d, ways)),
            device_id_type=MESH,
        )

    def rs_copy(unit, d):
        peer = lax.rem(me + d, ways)
        return pltpu.make_async_remote_copy(
            src_ref=sends.at[unit, peer],
            dst_ref=lands.at[unit, d - 1],
            send_sem=rs_send.at[unit, d - 1],
            recv_sem=rs_recv.at[unit, d - 1],
            device_id=(branch, dp, peer),
            device_id_type=MESH,
        )

    def own_hidden(unit):
        if unit == 2:
            return unet_hidden[0]
        half = 1 - branch if unit == 0 else branch
        return control_hidden[0, half, 0]

    for unit in range(3):
        gathered[unit, me] = norm_silu(own_hidden(unit).astype(jnp.float32)).astype(jnp.bfloat16)
        if unit == 0:
            pl.semaphore_wait(barrier, ways)
        for d in range(1, ways):
            ag_copy(unit, d, me).start()

    def block(unit, first_weight, second_weight, total, first_load, second_load):
        for d in range(1, ways):
            ag_copy(unit, d, lax.rem(me + ways - d, ways)).wait_recv()
        if first_load is not None:
            first_load.wait()
        half = 2 if unit == 2 else (1 - branch if unit == 0 else branch)
        inner[...] = jnp.broadcast_to(start[half][:, :1], (width, pixels))

        def first_tap(tap, carry):
            dy = tap // 3 - 1
            dx = lax.rem(tap, 3) - 1
            term = jnp.dot(
                first_weight[tap],
                gathered[unit].reshape(channels, pixels),
                preferred_element_type=jnp.float32,
            )
            moved = pltpu.roll(term, lax.rem(2 * pixels - (SIDE * dy + dx), pixels), 1)
            spot = lax.broadcasted_iota(jnp.int32, (1, pixels), 1)
            row = spot // SIDE + dy
            col = lax.rem(spot, SIDE) + dx
            keep = (row >= 0) & (row < SIDE) & (col >= 0) & (col < SIDE)
            inner[...] += jnp.where(keep, moved, 0.0)
            return carry

        lax.fori_loop(0, 9, first_tap, 0)
        flipped[...] = norm_silu(inner[...]).T
        if second_load is not None:
            second_load.wait()

        def second_tap(tap, carry):
            dy = tap // 3 - 1
            dx = lax.rem(tap, 3) - 1
            moved = pltpu.roll(flipped[...], lax.rem(2 * pixels - (SIDE * dy + dx), pixels), 0)
            spot = lax.broadcasted_iota(jnp.int32, (pixels, 1), 0)
            row = spot // SIDE + dy
            col = lax.rem(spot, SIDE) + dx
            keep = (row >= 0) & (row < SIDE) & (col >= 0) & (col < SIDE)
            operand = jnp.where(keep, moved, 0.0).astype(jnp.bfloat16)
            term = jnp.dot(operand, second_weight[tap], preferred_element_type=jnp.float32)

            @pl.when(tap == 0)
            def _():
                total[...] = term

            @pl.when(tap > 0)
            def _():
                total[...] += term

            return carry

        lax.fori_loop(0, 9, second_tap, 0)

    def scatter(unit, total):
        sends[unit] = total[...].T.astype(jnp.bfloat16).reshape(ways, width, pixels)
        for d in range(1, ways):
            rs_copy(unit, d).start()

    def collect(unit):
        summed = own_hidden(unit).astype(jnp.float32) + sends[unit, me].astype(jnp.float32)
        for d in range(1, ways):
            rs_copy(unit, d).wait_recv()
            summed = summed + lands[unit, d - 1].astype(jnp.float32)
        return summed

    block(0, w1c, w2c, total_c, loads[0], loads[1])
    scatter(0, total_c)
    block(1, w1c, w2c, total_c, None, None)
    scatter(1, total_c)
    block(2, w1u, w2u, total_u, loads[2], loads[3])

    def residual(unit):
        half = 1 - branch if unit == 0 else branch
        copy_out = collect(unit).T.astype(jnp.bfloat16)
        term = jnp.dot(copy_out, wz[...], preferred_element_type=jnp.float32)
        return term * scale[half][:1, :1]

    loads[4].wait()
    swap_out[...] = residual(0).astype(jnp.bfloat16)
    swap = pltpu.make_async_remote_copy(
        src_ref=swap_out,
        dst_ref=swap_in,
        send_sem=swap_send,
        recv_sem=swap_recv,
        device_id=(1 - branch, dp, me),
        device_id_type=MESH,
    )
    swap.start()
    total_u[...] += residual(1)
    swap.wait_recv()
    total_u[...] += swap_in[...].astype(jnp.float32)
    scatter(2, total_u)
    out[0] = collect(2).astype(jnp.bfloat16)
    swap.wait_send()
    for unit in range(3):
        for d in range(1, ways):
            ag_copy(unit, d, me).wait_send()
            rs_copy(unit, d).wait_send()


def shards(
    unet_hidden,
    control_hidden,
    timesteps,
    control_scales,
    unet_time_first,
    unet_time_second,
    unet_proj,
    unet_conv_first,
    unet_conv_second,
    control_time_first,
    control_time_second,
    control_proj,
    control_conv_first,
    control_conv_second,
    zero_conv,
):
    ways = lax.axis_size("mp")
    width, pixels = unet_hidden.shape[1], unet_hidden.shape[2]
    channels = ways * width
    halves = timesteps.shape[0]
    waves = sinusoid(timesteps.reshape(halves)).astype(jnp.bfloat16)
    own_wave = lax.dynamic_slice_in_dim(waves, lax.axis_index("branch"), 1, 0)
    start_u = jnp.dot(
        time_embed(own_wave, unet_time_first, unet_time_second),
        unet_proj,
        preferred_element_type=jnp.float32,
    )
    start_c = jnp.dot(
        time_embed(waves, control_time_first[0], control_time_second[0]),
        control_proj[0],
        preferred_element_type=jnp.float32,
    )
    start = jnp.concatenate([start_c, start_u], axis=0)
    start = jnp.broadcast_to(start[:, :, None], (halves + 1, width, 128))
    scale = control_scales[0].astype(jnp.float32) / 8.0
    scale = jnp.broadcast_to(scale[:, :, None], (halves, 8, 128))
    vmem = pl.BlockSpec(memory_space=pltpu.VMEM)
    hbm = pl.BlockSpec(memory_space=pl.ANY)
    taps = unet_conv_first.shape[0]
    bf16, f32 = jnp.bfloat16, jnp.float32
    conv_shape = (taps, width, channels)
    return pl.pallas_call(
        functools.partial(kernel, ways),
        out_shape=jax.ShapeDtypeStruct((1, width, pixels), bf16),
        in_specs=[vmem] * 4 + [hbm] * 5,
        out_specs=vmem,
        scratch_shapes=[
            pltpu.VMEM(conv_shape, bf16),
            pltpu.VMEM(conv_shape, bf16),
            pltpu.VMEM(conv_shape, bf16),
            pltpu.VMEM(conv_shape, bf16),
            pltpu.VMEM((width, channels), bf16),
            pltpu.VMEM((3, ways, width, pixels), bf16),
            pltpu.VMEM((width, pixels), f32),
            pltpu.VMEM((pixels, width), f32),
            pltpu.VMEM((pixels, channels), f32),
            pltpu.VMEM((pixels, channels), f32),
            pltpu.VMEM((3, ways, width, pixels), bf16),
            pltpu.VMEM((3, ways - 1, width, pixels), bf16),
            pltpu.VMEM((pixels, channels), bf16),
            pltpu.VMEM((pixels, channels), bf16),
            pltpu.SemaphoreType.DMA((5,)),
            pltpu.SemaphoreType.DMA((3, ways - 1)),
            pltpu.SemaphoreType.DMA((3, ways - 1)),
            pltpu.SemaphoreType.DMA((3, ways - 1)),
            pltpu.SemaphoreType.DMA((3, ways - 1)),
            pltpu.SemaphoreType.DMA,
            pltpu.SemaphoreType.DMA,
        ],
        compiler_params=pltpu.CompilerParams(
            collective_id=0, has_side_effects=True, vmem_limit_bytes=60 * 1024 * 1024
        ),
    )(
        unet_hidden,
        control_hidden,
        start,
        scale,
        unet_conv_first,
        unet_conv_second,
        control_conv_first[0],
        control_conv_second[0],
        zero_conv[0],
    )


def solution(mesh):
    in_specs = (
        P(("branch", "dp"), "mp", None),
        P("branch", None, "dp", "mp", None),
        P(None, "dp"),
        P("branch", None, "dp"),
        P(),
        P(),
        P(None, "mp"),
        P(None, "mp", None),
        P(None, "mp", None),
        P("branch", None, None),
        P("branch", None, None),
        P("branch", None, "mp"),
        P("branch", None, "mp", None),
        P("branch", None, "mp", None),
        P("branch", "mp", None),
    )
    out_specs = P(("branch", "dp"), "mp", None)
    return jax.shard_map(shards, mesh=mesh, in_specs=in_specs, out_specs=out_specs, check_vma=False)
```

time: 217 us -> 104 us (0.48)
  Pallas kernels: 0 us -> 90.8 us
  waiting for transfers between devices: 71.4 us -> 0 us
  matrix products: 60.6 us -> 6.68 us
  blocking collectives: 27.8 us -> 0 us
  local copies, waits for them, and re-layouts: 26.8 us -> 3.24 us
  between operations: 13.9 us -> 0.1 us
  other arithmetic: 15 us -> 1.84 us
    pallas_call x0 -> x1, Pallas kernels: none -> 90.8 us  [shards(): pl.pallas_call(functools.partial(kernel, ways), out_shape=jax.ShapeDtypeS...]
    reduce_scatter x3 -> x0, waiting for transfers between devices: 71.3 us -> none  [the longest x1 38.2 us: shards(): lax.psum_scatter(merged.astype(jnp.bfloat16), ('branch', 'mp'), scatter_d...]
    dot_general x39 -> x2, matrix products: 57.2 us -> 3.17 us  [the longest x1 2.89 us: shards(): jnp.dot(time_embed(waves, control_time_first[0], control_time_second[0]),...]
    all_gather x1 -> x0, blocking collectives: 27.8 us -> none  [resnet_block(): lax.all_gather(operand, 'mp', axis=1, tiled=True)]
    slice x4 -> x0, local copies, waits for them, and re-layouts: 16.7 us -> none  [conv_taps(): padded[:, :, row_shift:row_shift + SIDE, col_shift:col_shift + SIDE]]
    reduce_sum x14 -> x0, other arithmetic: 7.11 us -> none  [the longest x8 4.33 us: norm_silu(): group_var = jnp.mean(centered * centered, axis=(2, 3), keepdims=True)]
    convert_element_type x6 -> x0, other arithmetic: 6.87 us -> none  [the longest x2 3.11 us: resnet_block(): operand = norm_silu(hidden.astype(jnp.float32)).astype(jnp.bfloat16)]
    all_gather x2 -> x0, local copies, waits for them, and re-layouts: 4.63 us -> none  [resnet_block(): lax.all_gather(operand, 'mp', axis=1, tiled=True)]
  transfers between devices with their start and end apart: 4 -> 0, of which waited for: 3 -> 0; matrix products, arithmetic and copies ran while one was open for 30% -> 0% of each run, Pallas kernels for 0% -> 0%
where the time goes in v1:
time: 104 us; the launch traced here: 103 us
  Pallas kernels  90.8 us (87%)
  matrix products  6.68 us (6%)
  local copies, waits for them, and re-layouts  3.24 us (3%)
  other arithmetic  1.84 us (2%)
    pallas_call x1, Pallas kernels, shards(): pl.pallas_call(functools.partial(kernel, ways), out_shape=jax.ShapeDtypeS...  90.8 us
    dot_general x2, matrix products, time_embed(): jnp.dot(waves, first_weight, preferred_element_type=jnp.float32)  2.96 us
    dot_general x1, matrix products, shards(): jnp.dot(time_embed(waves, control_time_first[0], control_time_second[0]),...  2.89 us

profile of v1, /device:TPU:0, one launch (start us, length us, event | category | flops | bytes accessed | tf_op | source)
XLA Modules:
  0.0 102.6 jit_solution(11298557785967622948)
XLA Ops:
  0.0 0.0 copy-start
  0.0 0.8 convert_bitcast_fusion
  0.8 0.8 multiply_bitcast_fusion
  1.6 0.1 fusion.19
  1.8 1.4 %fusion.15 = bf16[2,1280]{1,0:T(2,128)(2,1)S(1)} fusion(bf16[1,320,1280]{2,1,0:T(8,128)(2,1)} %param.24, bf16[2,160]{1,0:T(2,128)(2,1)S(1)} %get-tuple-element.6, bf16[2,160]{1,0:T(2,128)(2,1)S(1)} %get-tuple-element.5), kind=kOutput, calls=%fused_computation.11 | convolution fusion | flops 1653760 | bytes 825600 | tf_op jit(solution)/shard_map/dot_general | solution.py:25
  3.2 2.9 %fusion.2 = f32[2,320]{1,0:T(2,128)S(1)} fusion(bf16[1,1280,320]{1,2,0:T(8,128)(2,1)} %param.26, bf16[2,1280]{1,0:T(2,128)(2,1)S(1)} %fusion.15, bf16[1,1280,1280]{2,1,0:T(8,128)(2,1)} %param.25), kind=kOutput, calls=%fused_computation.4 | convolution fusion | flops 8204800 | bytes 4103680 | tf_op jit(solution)/shard_map/dot_general | solution.py:260
  6.1 0.0 copy-start.1
  6.1 1.5 %convolution_reduce_fusion.1 = f32[1280]{0:T(1024)S(1)} fusion(bf16[320,1280]{1,0:T(8,128)(2,1)} %param.19, s32[]{:T(128)S(6)} %select_n.3, bf16[2,160]{1,0:T(2,128)(2,1)S(1)} %get-tuple-element.6, bf16[2,160]{1,0:T(2,128)(2,1)S(1)} %get-tuple-element.5), kind=kOutput, calls=%fused_computation.3 | convolution fusion | flops 820480 | bytes 825604 | tf_op jit(solution)/shard_map/dot_general | solution.py:25
  7.7 0.0 copy-done
  7.7 0.5 convolution_reduce_fusion
  8.3 0.0 copy-done.1
  8.3 0.3 fusion.32
  8.6 0.1 pad_maximum_fusion
  8.6 0.7 broadcast_in_dim.5.scale
  9.3 1.0 broadcast_in_dim.4.start
  10.3 90.8 %shard_map.145 = bf16[1,320,256]{2,1,0:T(8,128)(2,1)} custom-call(bf16[1,320,256]{2,1,0:T(8,128)(2,1)} %unet_hidden.1, bf16[1,2,1,320,256]{4,3,2,1,0:T(8,128)(2,1)} %control_hidden.1, f32[3,320,128]{2,1,0:T(8,128)} %broadcast_in_dim.4.start, f32[2,8,128]{2,1,0:T(8,128)} %broadcast_in_dim.5.scale, bf16[9,320,1280]{2,1,0:T(8,128)(2,1)} %first_u.1, ...), custom_call_target="tpu_custom_call" | custom-call | tf_op jit(solution)/shard_map/pallas_call | solution.py:274
  101.0 1.6 %copy.17 = bf16[1,320,256]{2,1,0:T(8,128)(2,1)} copy(bf16[1,320,256]{2,1,0:T(8,128)(2,1)} %shard_map.145) | data formatting | bytes 327680
  (5 shorter events, 0.0 us)
Async XLA Ops:
  0.0 7.7 %copy-start = (bf16[1280,1280]{1,0:T(8,128)(2,1)S(1)}, bf16[1280,1280]{1,0:T(8,128)(2,1)}, u32[]{:S(2)}) copy-start(bf16[1280,1280]{1,0:T(8,128)(2,1)} %param.20) | copy-start | bytes 9830404
  6.1 2.2 %copy-start.1 = (bf16[1280,320]{0,1:T(8,128)(2,1)S(1)}, bf16[1280,320]{0,1:T(8,128)(2,1)}, u32[]{:S(2)}) copy-start(bf16[1280,320]{0,1:T(8,128)(2,1)} %param.21) | copy-start | bytes 2457604

commit v2 on v1

v2 whole, which is shorter than its diff:
```python
import functools
import math

import jax
import jax.numpy as jnp
from jax import lax
from jax.experimental import pallas as pl
from jax.experimental.pallas import tpu as pltpu
from jax.sharding import PartitionSpec as P

TDIM = 320
GROUP = 40
SIDE = 16
MESH = pl.DeviceIdType.MESH


def sinusoid(step_ids):
    half_width = TDIM // 2
    frequency = jnp.exp(-math.log(10000.0) * jnp.arange(half_width, dtype=jnp.float32) / half_width)
    angles = step_ids.astype(jnp.float32)[:, None] * frequency[None, :]
    return jnp.concatenate([jnp.cos(angles), jnp.sin(angles)], axis=1)


def norm_silu(values):
    width, pixels = values.shape
    grouped = values.reshape(width // GROUP, GROUP, pixels)
    count = 1.0 / (GROUP * pixels)
    mean = jnp.sum(jnp.sum(grouped, axis=1, keepdims=True), axis=2, keepdims=True) * count
    centered = grouped - mean
    var = jnp.sum(jnp.sum(centered * centered, axis=1, keepdims=True), axis=2, keepdims=True) * count
    normed = centered * lax.rsqrt(var + 1e-05)
    return jax.nn.silu(normed).reshape(width, pixels)


def kernel(
    ways,
    unet_hidden,
    control_hidden,
    waves,
    scale,
    hbm_time_first_c,
    hbm_time_second_c,
    hbm_proj_c,
    hbm_time_first_u,
    hbm_time_second_u,
    hbm_proj_u,
    first_c,
    second_c,
    first_u,
    second_u,
    zero,
    out,
    time_first,
    time_second,
    proj,
    w1c,
    w2c,
    w1u,
    w2u,
    wz,
    gathered,
    start,
    inner,
    flipped,
    total_c,
    total_u,
    sends,
    lands,
    swap_out,
    swap_in,
    load_sem,
    ag_send,
    ag_recv,
    rs_send,
    rs_recv,
    swap_send,
    swap_recv,
):
    branch = lax.axis_index("branch")
    dp = lax.axis_index("dp")
    me = lax.axis_index("mp")
    width, pixels = unet_hidden.shape[1], unet_hidden.shape[2]
    channels = ways * width
    last = ways - 1

    loads = [
        pltpu.make_async_copy(src, dst, load_sem.at[i])
        for i, (src, dst) in enumerate(
            (
                (hbm_time_first_c, time_first.at[0]),
                (hbm_time_second_c, time_second.at[0]),
                (hbm_proj_c, proj.at[0]),
                (hbm_time_first_u, time_first.at[1]),
                (hbm_time_second_u, time_second.at[1]),
                (hbm_proj_u, proj.at[1]),
                (first_c, w1c),
                (second_c, w2c),
                (first_u, w1u),
                (second_u, w2u),
                (zero, wz),
            )
        )
    ]
    for load in loads:
        load.start()

    barrier = pltpu.get_barrier_semaphore()

    def greet(inside, coord):
        @pl.when(inside)
        def _():
            pl.semaphore_signal(barrier, inc=1, device_id=coord, device_id_type=MESH)

    greet(me < last, (branch, dp, me + 1))
    greet(me > 0, (branch, dp, me - 1))
    pl.semaphore_signal(barrier, inc=1, device_id=(1 - branch, dp, me), device_id_type=MESH)

    def wait_barrier():
        edge = (me == 0) | (me == last)

        @pl.when(edge)
        def _():
            pl.semaphore_wait(barrier, 2)

        @pl.when(jnp.logical_not(edge))
        def _():
            pl.semaphore_wait(barrier, 3)

    def ag_copy(unit, side, hop, slot):
        return pltpu.make_async_remote_copy(
            src_ref=gathered.at[unit, slot],
            dst_ref=gathered.at[unit, slot],
            send_sem=ag_send.at[unit, side, hop],
            recv_sem=ag_recv.at[unit, side, hop],
            device_id=(branch, dp, me + 1 - 2 * side),
            device_id_type=MESH,
        )

    def ag_step(unit, hop, waits=True, sends_on=True):
        for side in range(2):
            from_slot = me - hop if side == 0 else me + hop
            here = (from_slot >= 0) & (from_slot <= last)
            onward = here & ((me < last) if side == 0 else (me > 0))

            if waits:

                @pl.when(here)
                def _():
                    ag_copy(unit, side, hop - 1, from_slot).wait_recv()

            if sends_on:

                @pl.when(onward)
                def _():
                    ag_copy(unit, side, hop, from_slot).start()

    def ag_drain(unit):
        for hop in range(last):
            for side in range(2):
                from_slot = me - hop if side == 0 else me + hop
                here = (from_slot >= 0) & (from_slot <= last)
                onward = here & ((me < last) if side == 0 else (me > 0))

                @pl.when(onward)
                def _():
                    ag_copy(unit, side, hop, from_slot).wait_send()

    def rs_copy(unit, side, dest):
        return pltpu.make_async_remote_copy(
            src_ref=sends.at[unit, dest],
            dst_ref=lands.at[unit, side, dest],
            send_sem=rs_send.at[unit, dest],
            recv_sem=rs_recv.at[unit, side, dest],
            device_id=(branch, dp, me + 1 - 2 * side),
            device_id_type=MESH,
        )

    def rs_start(unit):
        @pl.when(me == 0)
        def _():
            for dest in range(last, 0, -1):
                rs_copy(unit, 0, dest).start()

        @pl.when(me == last)
        def _():
            for dest in range(last):
                rs_copy(unit, 1, dest).start()

    def rs_slot(unit, slot):
        for side in range(2):
            place = me if side == 0 else last - me
            dest = last - slot + place if side == 0 else slot - place

            @pl.when((place >= 1) & (place <= slot))
            def _():
                rs_copy(unit, side, dest).wait_recv()
                added = sends[unit, dest].astype(jnp.float32) + lands[unit, side, dest].astype(
                    jnp.float32
                )
                sends[unit, dest] = added.astype(jnp.bfloat16)
                rs_copy(unit, side, dest).start()

    def rs_drain(unit):
        for dest in range(ways):

            @pl.when(dest > me)
            def _():
                rs_copy(unit, 0, dest).wait_send()

            @pl.when(dest < me)
            def _():
                rs_copy(unit, 1, dest).wait_send()

    def own_hidden(unit):
        if unit == 2:
            return unet_hidden[0]
        half = 1 - branch if unit == 0 else branch
        return control_hidden[0, half, 0]

    def prepare(unit):
        gathered[unit, me] = norm_silu(own_hidden(unit).astype(jnp.float32)).astype(jnp.bfloat16)

    def embed(block):
        for load in loads[3 * block : 3 * block + 3]:
            load.wait()
        act = waves[...]
        for weight in (time_first, time_second):
            act = jax.nn.silu(
                jnp.dot(act, weight[block], preferred_element_type=jnp.float32)
            ).astype(jnp.bfloat16)
        start[block] = jnp.dot(act, proj[block], preferred_element_type=jnp.float32).T

    def keep_of(tap, shape, axis):
        dy = tap // 3 - 1
        dx = lax.rem(tap, 3) - 1
        spot = lax.broadcasted_iota(jnp.int32, shape, axis)
        row = spot // SIDE + dy
        col = lax.rem(spot, SIDE) + dx
        keep = (row >= 0) & (row < SIDE) & (col >= 0) & (col < SIDE)
        return keep, lax.rem(2 * pixels - (SIDE * dy + dx), pixels)

    def block(unit, first_weight, second_weight, total, first_load, second_load, hooks):
        ag_step(unit, last, sends_on=False)
        if first_load is not None:
            first_load.wait()
        row = 0 if unit == 0 else 1
        inner[...] = jnp.broadcast_to(start[unit // 2][:, row : row + 1], (width, pixels))

        def run(step):
            for place, hook in hooks:
                pl.when(step == place)(hook)

        def first_tap(tap, carry):
            run(tap)
            term = jnp.dot(
                first_weight[tap],
                gathered[unit].reshape(channels, pixels),
                preferred_element_type=jnp.float32,
            )
            keep, shift = keep_of(tap, (1, pixels), 1)
            inner[...] += jnp.where(keep, pltpu.roll(term, shift, 1), 0.0)
            return carry

        lax.fori_loop(0, 9, first_tap, 0)
        flipped[...] = norm_silu(inner[...]).T
        if second_load is not None:
            second_load.wait()
        total[...] = jnp.zeros_like(total)

        def second_tap(tap, carry):
            run(tap + 9)
            keep, shift = keep_of(tap, (pixels, 1), 0)
            operand = jnp.where(keep, pltpu.roll(flipped[...], shift, 0), 0.0).astype(jnp.bfloat16)
            total[...] += jnp.dot(operand, second_weight[tap], preferred_element_type=jnp.float32)
            return carry

        lax.fori_loop(0, 9, second_tap, 0)

    def scatter(unit, total):
        sends[unit] = total[...].T.astype(jnp.bfloat16).reshape(ways, width, pixels)
        rs_start(unit)

    def collect(unit):
        inner[...] = own_hidden(unit).astype(jnp.float32) + sends[unit, me].astype(jnp.float32)
        for side, inside in ((0, me > 0), (1, me < last)):

            @pl.when(inside)
            def _():
                rs_copy(unit, side, me).wait_recv()
                inner[...] += lands[unit, side, me].astype(jnp.float32)

        return inner[...]

    def residual(unit):
        half = 1 - branch if unit == 0 else branch
        copy_out = collect(unit).T.astype(jnp.bfloat16)
        term = jnp.dot(copy_out, wz[...], preferred_element_type=jnp.float32)
        return term * scale[half][:1, :1]

    def spread(first, span, count):
        return [first + i * span // max(count, 1) for i in range(count)]

    prepare(0)
    wait_barrier()
    ag_step(0, 0, waits=False)
    prepare(1)
    prepare(2)
    relays = range(1, last)
    for hop in relays:
        ag_step(0, hop)
        if hop == 1:
            embed(0)
    ag_step(1, 0, waits=False)
    embed(1)

    def relay_hook(unit, hop):
        def hook():
            ag_step(unit, hop)
            if unit == 1 and hop == last - 1:
                ag_step(2, 0, waits=False)

        return hook

    def slot_hook(unit, slot):
        return lambda: rs_slot(unit, slot)

    block(
        0, w1c, w2c, total_c, loads[6], loads[7],
        [(p, relay_hook(1, h)) for p, h in zip(spread(4, 12, len(relays)), relays)],
    )
    scatter(0, total_c)
    block(
        1, w1c, w2c, total_c, None, None,
        [(p, relay_hook(2, h)) for p, h in zip(spread(1, 12, len(relays)), relays)]
        + [(p, slot_hook(0, k)) for p, k in zip(spread(8, 10, len(relays)), relays)],
    )
    scatter(1, total_c)
    block(
        2, w1u, w2u, total_u, loads[8], loads[9],
        [(p, slot_hook(1, k)) for p, k in zip(spread(6, 12, len(relays)), relays)],
    )
    loads[10].wait()
    swap_out[...] = residual(0).astype(jnp.bfloat16)
    swap = pltpu.make_async_remote_copy(
        src_ref=swap_out,
        dst_ref=swap_in,
        send_sem=swap_send,
        recv_sem=swap_recv,
        device_id=(1 - branch, dp, me),
        device_id_type=MESH,
    )
    swap.start()
    total_u[...] += residual(1)
    swap.wait_recv()
    total_u[...] += swap_in[...].astype(jnp.float32)
    scatter(2, total_u)
    for slot in relays:
        rs_slot(2, slot)
    out[0] = collect(2).astype(jnp.bfloat16)
    swap.wait_send()
    for unit in range(3):
        ag_drain(unit)
        rs_drain(unit)


def shards(
    unet_hidden,
    control_hidden,
    timesteps,
    control_scales,
    unet_time_first,
    unet_time_second,
    unet_proj,
    unet_conv_first,
    unet_conv_second,
    control_time_first,
    control_time_second,
    control_proj,
    control_conv_first,
    control_conv_second,
    zero_conv,
):
    ways = lax.axis_size("mp")
    width, pixels = unet_hidden.shape[1], unet_hidden.shape[2]
    channels = ways * width
    halves = timesteps.shape[0]
    branch = lax.axis_index("branch")
    steps = timesteps.reshape(halves)
    waves = sinusoid(jnp.stack([steps[1 - branch], steps[branch]])).astype(jnp.bfloat16)
    waves = jnp.pad(waves, ((0, 16 - halves), (0, 0)))
    scale = control_scales[0].astype(jnp.float32) / 8.0
    scale = jnp.broadcast_to(scale[:, :, None], (halves, 8, 128))
    vmem = pl.BlockSpec(memory_space=pltpu.VMEM)
    hbm = pl.BlockSpec(memory_space=pl.ANY)
    taps = unet_conv_first.shape[0]
    bf16, f32 = jnp.bfloat16, jnp.float32
    conv_shape = (taps, width, channels)
    return pl.pallas_call(
        functools.partial(kernel, ways),
        out_shape=jax.ShapeDtypeStruct((1, width, pixels), bf16),
        in_specs=[vmem] * 4 + [hbm] * 11,
        out_specs=vmem,
        scratch_shapes=[
            pltpu.VMEM((2,) + unet_time_first.shape, bf16),
            pltpu.VMEM((2,) + unet_time_second.shape, bf16),
            pltpu.VMEM((2,) + unet_proj.shape, bf16),
            pltpu.VMEM(conv_shape, bf16),
            pltpu.VMEM(conv_shape, bf16),
            pltpu.VMEM(conv_shape, bf16),
            pltpu.VMEM(conv_shape, bf16),
            pltpu.VMEM((width, channels), bf16),
            pltpu.VMEM((3, ways, width, pixels), bf16),
            pltpu.VMEM((2, width, 16), f32),
            pltpu.VMEM((width, pixels), f32),
            pltpu.VMEM((pixels, width), f32),
            pltpu.VMEM((pixels, channels), f32),
            pltpu.VMEM((pixels, channels), f32),
            pltpu.VMEM((3, ways, width, pixels), bf16),
            pltpu.VMEM((3, 2, ways, width, pixels), bf16),
            pltpu.VMEM((pixels, channels), bf16),
            pltpu.VMEM((pixels, channels), bf16),
            pltpu.SemaphoreType.DMA((11,)),
            pltpu.SemaphoreType.DMA((3, 2, ways - 1)),
            pltpu.SemaphoreType.DMA((3, 2, ways - 1)),
            pltpu.SemaphoreType.DMA((3, ways)),
            pltpu.SemaphoreType.DMA((3, 2, ways)),
            pltpu.SemaphoreType.DMA,
            pltpu.SemaphoreType.DMA,
        ],
        compiler_params=pltpu.CompilerParams(
            collective_id=0, has_side_effects=True, vmem_limit_bytes=62 * 1024 * 1024
        ),
    )(
        unet_hidden,
        control_hidden,
        waves,
        scale,
        control_time_first[0],
        control_time_second[0],
        control_proj[0],
        unet_time_first,
        unet_time_second,
        unet_proj,
        control_conv_first[0],
        control_conv_second[0],
        unet_conv_first,
        unet_conv_second,
        zero_conv[0],
    )


def solution(mesh):
    in_specs = (
        P(("branch", "dp"), "mp", None),
        P("branch", None, "dp", "mp", None),
        P(None, "dp"),
        P("branch", None, "dp"),
        P(),
        P(),
        P(None, "mp"),
        P(None, "mp", None),
        P(None, "mp", None),
        P("branch", None, None),
        P("branch", None, None),
        P("branch", None, "mp"),
        P("branch", None, "mp", None),
        P("branch", None, "mp", None),
        P("branch", "mp", None),
    )
    out_specs = P(("branch", "dp"), "mp", None)
    return jax.shard_map(shards, mesh=mesh, in_specs=in_specs, out_specs=out_specs, check_vma=False)
```

time: 104 us -> 89.1 us (0.86); the launches traced: 103 us -> 88.9 us
  Pallas kernels: 90.8 us -> 78 us
  matrix products: 6.68 us -> 0 us
  local copies, waits for them, and re-layouts: 3.24 us -> 8.03 us
    pallas_call x1, Pallas kernels: 90.8 us -> 78 us  [shards(): pl.pallas_call(functools.partial(kernel, ways), out_shape=jax.ShapeDtypeS...]
    dot_general x5 -> x0, matrix products: 6.68 us -> none  [the longest x2 2.96 us: time_embed(): jnp.dot(waves, first_weight, preferred_element_type=jnp.float32)]
    unnamed x5 -> x3, local copies, waits for them, and re-layouts: 1.6 us -> 6.02 us
    dynamic_slice x0 -> x1, local copies, waits for them, and re-layouts: none -> 1.34 us  [shards(): steps[1 - branch]]
    convert_element_type x2 -> x1, other arithmetic: 0.02 us -> 1.35 us  [sinusoid(): angles = step_ids.astype(jnp.float32)[:, None] * frequency[None, :]]
where the time goes in v2:
time: 89.1 us; the launch traced here: 88.9 us
  Pallas kernels  78 us (88%)
  local copies, waits for them, and re-layouts  8.03 us (9%)
  other arithmetic  2.82 us (3%)
    pallas_call x1, Pallas kernels, shards(): pl.pallas_call(functools.partial(kernel, ways), out_shape=jax.ShapeDtypeS...  78 us
    unnamed x3, local copies, waits for them, and re-layouts  6.02 us

profile of v2, /device:TPU:0, one launch (start us, length us, event | category | flops | bytes accessed | tf_op | source)
XLA Modules:
  0.0 88.9 jit_solution(8907787647174476131)
XLA Ops:
  0.0 1.3 %constant_dynamic-slice_fusion.1 = (s32[1,1]{0,1:T(1,128)}, s32[1,1]{0,1:T(1,128)}) fusion(s32[2,1]{0,1:T(1,128)} %param.17, s32[]{:T(128)S(6)} %select_n.6, s32[]{:T(128)S(6)} %select_n.7), kind=kLoop, calls=%fused_computation.12 | loop fusion | bytes 24 | tf_op jit(solution)/shard_map/dynamic_slice | solution.py:389
  1.3 1.4 %add_convert_fusion = f32[2]{0:T(128)S(1)} fusion(s32[1]{0:T(128)} %bitcast.1, s32[1]{0:T(128)} %bitcast), kind=kLoop, calls=%fused_computation.9 | loop fusion | flops 4 | bytes 16 | tf_op jit(solution)/shard_map/convert_element_type | solution.py:20
  2.7 0.7 multiply_bitcast_fusion
  3.4 0.1 fusion.3
  3.5 0.7 broadcast_in_dim.2.scale
  4.2 0.7 fusion.2.waves
  4.8 2.2 %copy.17.hbm_proj_u = bf16[1280,320]{1,0:T(8,128)(2,1)} copy(bf16[1280,320]{0,1:T(8,128)(2,1)} %param.21) | data formatting | bytes 1638400 | tf_op args[6]
  7.0 2.2 %copy.16 = bf16[1,1280,320]{2,1,0:T(8,128)(2,1)} copy(bf16[1,1280,320]{1,2,0:T(8,128)(2,1)} %param.26) | data formatting | bytes 1638400 | tf_op args[11]
  9.3 78.0 %shard_map.145 = bf16[1,320,256]{2,1,0:T(8,128)(2,1)} custom-call(bf16[1,320,256]{2,1,0:T(8,128)(2,1)} %unet_hidden.1, bf16[1,2,1,320,256]{4,3,2,1,0:T(8,128)(2,1)} %control_hidden.1, bf16[16,320]{1,0:T(8,128)(2,1)} %fusion.2.waves, f32[2,8,128]{2,1,0:T(8,128)} %broadcast_in_dim.2.scale, bf16[320,1280]{1,0:T(8,128)(2,1)} %bitcast.14, ...), custom_call_target="tpu_custom_call" | custom-call | tf_op jit(solution)/shard_map/pallas_call | solution.py:398
  87.3 1.6 %copy.19 = bf16[1,320,256]{2,1,0:T(8,128)(2,1)} copy(bf16[1,320,256]{2,1,0:T(8,128)(2,1)} %shard_map.145) | data formatting | bytes 327680
  (1 shorter events, 0.0 us)

commit v3 on v2

--- a/solution.py
+++ b/solution.py
@@ -10,6 +10,7 @@
 
 TDIM = 320
 GROUP = 40
+PIECES = 2
 SIDE = 16
 MESH = pl.DeviceIdType.MESH
 
@@ -126,18 +127,21 @@
         def _():
             pl.semaphore_wait(barrier, 3)
 
-    def ag_copy(unit, side, hop, slot):
+    def part(piece):
+        return pl.ds(piece * (pixels // PIECES), pixels // PIECES)
+
+    def ag_copy(unit, side, hop, slot, piece):
         return pltpu.make_async_remote_copy(
-            src_ref=gathered.at[unit, slot],
-            dst_ref=gathered.at[unit, slot],
-            send_sem=ag_send.at[unit, side, hop],
-            recv_sem=ag_recv.at[unit, side, hop],
+            src_ref=gathered.at[unit, slot, :, part(piece)],
+            dst_ref=gathered.at[unit, slot, :, part(piece)],
+            send_sem=ag_send.at[unit, side, hop, piece],
+            recv_sem=ag_recv.at[unit, side, hop, piece],
             device_id=(branch, dp, me + 1 - 2 * side),
             device_id_type=MESH,
         )
 
     def ag_step(unit, hop, waits=True, sends_on=True):
-        for side in range(2):
+        for piece, side in [(p, d) for p in range(PIECES) for d in range(2)]:
             from_slot = me - hop if side == 0 else me + hop
             here = (from_slot >= 0) & (from_slot <= last)
             onward = here & ((me < last) if side == 0 else (me > 0))
@@ -146,13 +150,13 @@
 
                 @pl.when(here)
                 def _():
-                    ag_copy(unit, side, hop - 1, from_slot).wait_recv()
+                    ag_copy(unit, side, hop - 1, from_slot, piece).wait_recv()
 
             if sends_on:
 
                 @pl.when(onward)
                 def _():
-                    ag_copy(unit, side, hop, from_slot).start()
+                    ag_copy(unit, side, hop, from_slot, piece).start()
 
     def ag_drain(unit):
         for hop in range(last):
@@ -163,14 +167,15 @@
 
                 @pl.when(onward)
                 def _():
-                    ag_copy(unit, side, hop, from_slot).wait_send()
-
-    def rs_copy(unit, side, dest):
+                    for piece in range(PIECES):
+                        ag_copy(unit, side, hop, from_slot, piece).wait_send()
+
+    def rs_copy(unit, side, dest, piece):
         return pltpu.make_async_remote_copy(
-            src_ref=sends.at[unit, dest],
-            dst_ref=lands.at[unit, side, dest],
-            send_sem=rs_send.at[unit, dest],
-            recv_sem=rs_recv.at[unit, side, dest],
+            src_ref=sends.at[unit, dest, :, part(piece)],
+            dst_ref=lands.at[unit, side, dest, :, part(piece)],
+            send_sem=rs_send.at[unit, dest, piece],
+            recv_sem=rs_recv.at[unit, side, dest, piece],
             device_id=(branch, dp, me + 1 - 2 * side),
             device_id_type=MESH,
         )
@@ -179,37 +184,41 @@
         @pl.when(me == 0)
         def _():
             for dest in range(last, 0, -1):
-                rs_copy(unit, 0, dest).start()
+                for piece in range(PIECES):
+                    rs_copy(unit, 0, dest, piece).start()
 
         @pl.when(me == last)
         def _():
             for dest in range(last):
-                rs_copy(unit, 1, dest).start()
+                for piece in range(PIECES):
+                    rs_copy(unit, 1, dest, piece).start()
 
     def rs_slot(unit, slot):
-        for side in range(2):
+        for piece, side in [(p, d) for p in range(PIECES) for d in range(2)]:
             place = me if side == 0 else last - me
             dest = last - slot + place if side == 0 else slot - place
 
             @pl.when((place >= 1) & (place <= slot))
             def _():
-                rs_copy(unit, side, dest).wait_recv()
-                added = sends[unit, dest].astype(jnp.float32) + lands[unit, side, dest].astype(
-                    jnp.float32
-                )
-                sends[unit, dest] = added.astype(jnp.bfloat16)
-                rs_copy(unit, side, dest).start()
+                rs_copy(unit, side, dest, piece).wait_recv()
+                added = sends[unit, dest, :, part(piece)].astype(jnp.float32) + lands[
+                    unit, side, dest, :, part(piece)
+                ].astype(jnp.float32)
+                sends[unit, dest, :, part(piece)] = added.astype(jnp.bfloat16)
+                rs_copy(unit, side, dest, piece).start()
 
     def rs_drain(unit):
         for dest in range(ways):
 
             @pl.when(dest > me)
             def _():
-                rs_copy(unit, 0, dest).wait_send()
+                for piece in range(PIECES):
+                    rs_copy(unit, 0, dest, piece).wait_send()
 
             @pl.when(dest < me)
             def _():
-                rs_copy(unit, 1, dest).wait_send()
+                for piece in range(PIECES):
+                    rs_copy(unit, 1, dest, piece).wait_send()
 
     def own_hidden(unit):
         if unit == 2:
@@ -228,7 +237,9 @@
             act = jax.nn.silu(
                 jnp.dot(act, weight[block], preferred_element_type=jnp.float32)
             ).astype(jnp.bfloat16)
-        start[block] = jnp.dot(act, proj[block], preferred_element_type=jnp.float32).T
+        start[block] = lax.dot_general(
+            proj[block], act, (((1,), (1,)), ((), ())), preferred_element_type=jnp.float32
+        )
 
     def keep_of(tap, shape, axis):
         dy = tap // 3 - 1
@@ -243,8 +254,11 @@
         ag_step(unit, last, sends_on=False)
         if first_load is not None:
             first_load.wait()
-        row = 0 if unit == 0 else 1
-        inner[...] = jnp.broadcast_to(start[unit // 2][:, row : row + 1], (width, pixels))
+        other = branch == 1 if unit == 0 else branch == 0
+        columns = start[unit // 2]
+        inner[...] = jnp.broadcast_to(
+            jnp.where(other, columns[:, :1], columns[:, 1:2]), (width, pixels)
+        )
 
         def run(step):
             for place, hook in hooks:
@@ -286,7 +300,8 @@
 
             @pl.when(inside)
             def _():
-                rs_copy(unit, side, me).wait_recv()
+                for piece in range(PIECES):
+                    rs_copy(unit, side, me, piece).wait_recv()
                 inner[...] += lands[unit, side, me].astype(jnp.float32)
 
         return inner[...]
@@ -295,7 +310,7 @@
         half = 1 - branch if unit == 0 else branch
         copy_out = collect(unit).T.astype(jnp.bfloat16)
         term = jnp.dot(copy_out, wz[...], preferred_element_type=jnp.float32)
-        return term * scale[half][:1, :1]
+        return term * (scale[half, 0].astype(jnp.float32) * 0.125)
 
     def spread(first, span, count):
         return [first + i * span // max(count, 1) for i in range(count)]
@@ -335,10 +350,6 @@
         + [(p, slot_hook(0, k)) for p, k in zip(spread(8, 10, len(relays)), relays)],
     )
     scatter(1, total_c)
-    block(
-        2, w1u, w2u, total_u, loads[8], loads[9],
-        [(p, slot_hook(1, k)) for p, k in zip(spread(6, 12, len(relays)), relays)],
-    )
     loads[10].wait()
     swap_out[...] = residual(0).astype(jnp.bfloat16)
     swap = pltpu.make_async_remote_copy(
@@ -350,6 +361,10 @@
         device_id_type=MESH,
     )
     swap.start()
+    block(
+        2, w1u, w2u, total_u, loads[8], loads[9],
+        [(p, slot_hook(1, k)) for p, k in zip(spread(6, 12, len(relays)), relays)],
+    )
     total_u[...] += residual(1)
     swap.wait_recv()
     total_u[...] += swap_in[...].astype(jnp.float32)
@@ -384,12 +399,9 @@
     width, pixels = unet_hidden.shape[1], unet_hidden.shape[2]
     channels = ways * width
     halves = timesteps.shape[0]
-    branch = lax.axis_index("branch")
-    steps = timesteps.reshape(halves)
-    waves = sinusoid(jnp.stack([steps[1 - branch], steps[branch]])).astype(jnp.bfloat16)
+    waves = sinusoid(timesteps.reshape(halves)).astype(jnp.bfloat16)
     waves = jnp.pad(waves, ((0, 16 - halves), (0, 0)))
-    scale = control_scales[0].astype(jnp.float32) / 8.0
-    scale = jnp.broadcast_to(scale[:, :, None], (halves, 8, 128))
+    scale = control_scales[0]
     vmem = pl.BlockSpec(memory_space=pltpu.VMEM)
     hbm = pl.BlockSpec(memory_space=pl.ANY)
     taps = unet_conv_first.shape[0]
@@ -398,12 +410,12 @@
     return pl.pallas_call(
         functools.partial(kernel, ways),
         out_shape=jax.ShapeDtypeStruct((1, width, pixels), bf16),
-        in_specs=[vmem] * 4 + [hbm] * 11,
+        in_specs=[vmem] * 3 + [pl.BlockSpec(memory_space=pltpu.SMEM)] + [hbm] * 11,
         out_specs=vmem,
         scratch_shapes=[
             pltpu.VMEM((2,) + unet_time_first.shape, bf16),
             pltpu.VMEM((2,) + unet_time_second.shape, bf16),
-            pltpu.VMEM((2,) + unet_proj.shape, bf16),
+            pltpu.VMEM((2,) + unet_proj.shape[::-1], bf16),
             pltpu.VMEM(conv_shape, bf16),
             pltpu.VMEM(conv_shape, bf16),
             pltpu.VMEM(conv_shape, bf16),
@@ -420,10 +432,10 @@
             pltpu.VMEM((pixels, channels), bf16),
             pltpu.VMEM((pixels, channels), bf16),
             pltpu.SemaphoreType.DMA((11,)),
-            pltpu.SemaphoreType.DMA((3, 2, ways - 1)),
-            pltpu.SemaphoreType.DMA((3, 2, ways - 1)),
-            pltpu.SemaphoreType.DMA((3, ways)),
-            pltpu.SemaphoreType.DMA((3, 2, ways)),
+            pltpu.SemaphoreType.DMA((3, 2, ways - 1, PIECES)),
+            pltpu.SemaphoreType.DMA((3, 2, ways - 1, PIECES)),
+            pltpu.SemaphoreType.DMA((3, ways, PIECES)),
+            pltpu.SemaphoreType.DMA((3, 2, ways, PIECES)),
             pltpu.SemaphoreType.DMA,
             pltpu.SemaphoreType.DMA,
         ],
@@ -437,10 +449,10 @@
         scale,
         control_time_first[0],
         control_time_second[0],
-        control_proj[0],
+        control_proj[0].T,
         unet_time_first,
         unet_time_second,
-        unet_proj,
+        unet_proj.T,
         control_conv_first[0],
         control_conv_second[0],
         unet_conv_first,

time: 89.1 us -> 76.5 us (0.86)
  Pallas kernels: 78 us -> 72 us
  local copies, waits for them, and re-layouts: 8.03 us -> 2.87 us
  other arithmetic: 2.82 us -> 1.47 us
    pallas_call x1, Pallas kernels: 78 us -> 72 us  [shards(): pl.pallas_call(functools.partial(kernel, ways), out_shape=jax.ShapeDtypeS...]
    unnamed x3 -> x1, local copies, waits for them, and re-layouts: 6.02 us -> 1.59 us
    convert_element_type x1 -> x0, other arithmetic: 1.35 us -> none  [sinusoid(): angles = step_ids.astype(jnp.float32)[:, None] * frequency[None, :]]
    dynamic_slice x1 -> x0, local copies, waits for them, and re-layouts: 1.34 us -> none  [shards(): steps[1 - branch]]
    squeeze x0 -> x1, local copies, waits for them, and re-layouts: none -> 1.28 us  [shards(): scale = control_scales[0]]
where the time goes in v3:
time: 76.5 us; the launch traced here: 76.4 us
  Pallas kernels  72 us (94%)
  local copies, waits for them, and re-layouts  2.87 us (4%)
  other arithmetic  1.47 us (2%)
    pallas_call x1, Pallas kernels, shards(): pl.pallas_call(functools.partial(kernel, ways), out_shape=jax.ShapeDtypeS...  72 us
    unnamed x1, local copies, waits for them, and re-layouts  1.59 us

profile of v3, /device:TPU:0, one launch (start us, length us, event | category | flops | bytes accessed | tf_op | source)
XLA Modules:
  0.0 76.4 jit_solution(11638690523432274973)
XLA Ops:
  0.0 0.7 convert_bitcast_fusion
  0.7 1.3 %copy.16.scale = s32[2,1]{1,0:T(2,128)} copy(s32[2,1]{0,1:T(1,128)} %bitcast.19) | data formatting | bytes 16 | tf_op jit(solution)/shard_map/squeeze | solution.py:404
  1.9 0.1 fusion.3
  2.1 0.7 fusion.2.waves
  2.8 72.0 %shard_map.145 = bf16[1,320,256]{2,1,0:T(8,128)(2,1)} custom-call(bf16[1,320,256]{2,1,0:T(8,128)(2,1)} %unet_hidden.1, bf16[1,2,1,320,256]{4,3,2,1,0:T(8,128)(2,1)} %control_hidden.1, bf16[16,320]{1,0:T(8,128)(2,1)} %fusion.2.waves, s32[2,1]{1,0:T(2,128)} %copy.16.scale, bf16[320,1280]{1,0:T(8,128)(2,1)} %bitcast.15, bf16[1280,1280]{1,0:T(8,128)(2,1)} %bitcast.14, ...), custom_call_target="tpu_custom_call" | custom-call | tf_op jit(solution)/shard_map/pallas_call | solution.py:410
  74.8 1.6 %copy.18 = bf16[1,320,256]{2,1,0:T(8,128)(2,1)} copy(bf16[1,320,256]{2,1,0:T(8,128)(2,1)} %shard_map.145) | data formatting | bytes 327680
  (1 shorter events, 0.0 us)

commit v4 on v3

--- a/solution.py
+++ b/solution.py
@@ -281,14 +281,22 @@
             second_load.wait()
         total[...] = jnp.zeros_like(total)
 
-        def second_tap(tap, carry):
-            run(tap + 9)
-            keep, shift = keep_of(tap, (pixels, 1), 0)
-            operand = jnp.where(keep, pltpu.roll(flipped[...], shift, 0), 0.0).astype(jnp.bfloat16)
-            total[...] += jnp.dot(operand, second_weight[tap], preferred_element_type=jnp.float32)
+        def second_line(line, carry):
+            operands = []
+            for side in range(3):
+                tap = 3 * line + side
+                run(tap + 9)
+                keep, shift = keep_of(tap, (pixels, 1), 0)
+                moved = pltpu.roll(flipped[...], shift, 0)
+                operands.append(jnp.where(keep, moved, 0.0).astype(jnp.bfloat16))
+            total[...] += jnp.dot(
+                jnp.concatenate(operands, axis=1),
+                second_weight[pl.ds(3 * line, 3)].reshape(3 * width, channels),
+                preferred_element_type=jnp.float32,
+            )
             return carry
 
-        lax.fori_loop(0, 9, second_tap, 0)
+        lax.fori_loop(0, 3, second_line, 0)
 
     def scatter(unit, total):
         sends[unit] = total[...].T.astype(jnp.bfloat16).reshape(ways, width, pixels)

time: 76.5 us -> 74.8 us (0.978)
  Pallas kernels: 72 us -> 70.3 us
    pallas_call x1, Pallas kernels: 72 us -> 70.3 us  [shards(): pl.pallas_call(functools.partial(kernel, ways), out_shape=jax.ShapeDtypeS...]
where the time goes in v4:
time: 74.8 us; the launch traced here: 74.7 us
  Pallas kernels  70.3 us (94%)
  local copies, waits for them, and re-layouts  2.87 us (4%)
  other arithmetic  1.47 us (2%)
    pallas_call x1, Pallas kernels, shards(): pl.pallas_call(functools.partial(kernel, ways), out_shape=jax.ShapeDtypeS...  70.3 us
    unnamed x1, local copies, waits for them, and re-layouts  1.59 us

profile of v4, /device:TPU:0, one launch (start us, length us, event | category | flops | bytes accessed | tf_op | source)
XLA Modules:
  0.0 74.7 jit_solution(12606257228831687075)
XLA Ops:
  0.0 0.7 convert_bitcast_fusion
  0.7 1.3 %copy.16.scale = s32[2,1]{1,0:T(2,128)} copy(s32[2,1]{0,1:T(1,128)} %bitcast.19) | data formatting | bytes 16 | tf_op jit(solution)/shard_map/squeeze | solution.py:412
  1.9 0.1 fusion.3
  2.1 0.7 fusion.2.waves
  2.8 70.3 %shard_map.145 = bf16[1,320,256]{2,1,0:T(8,128)(2,1)} custom-call(bf16[1,320,256]{2,1,0:T(8,128)(2,1)} %unet_hidden.1, bf16[1,2,1,320,256]{4,3,2,1,0:T(8,128)(2,1)} %control_hidden.1, bf16[16,320]{1,0:T(8,128)(2,1)} %fusion.2.waves, s32[2,1]{1,0:T(2,128)} %copy.16.scale, bf16[320,1280]{1,0:T(8,128)(2,1)} %bitcast.15, bf16[1280,1280]{1,0:T(8,128)(2,1)} %bitcast.14, ...), custom_call_target="tpu_custom_call" | custom-call | tf_op jit(solution)/shard_map/pallas_call | solution.py:418
  73.1 1.6 %copy.18 = bf16[1,320,256]{2,1,0:T(8,128)(2,1)} copy(bf16[1,320,256]{2,1,0:T(8,128)(2,1)} %shard_map.145) | data formatting | bytes 327680
  (1 shorter events, 0.0 us)
